TPU v7x, 32 devices: a whole 2x2x4 slice. The times are simulated.
32 devices in a mesh: row: 4 (over x, core), col: 8 (over z, y).
Axes of the slice: x: 2, y: 2, z: 4, core: 2. Of those that a mesh axis runs over, the one named last changes fastest.
Arguments:
- normed: bfloat16 [12288, 6144], P(('row', 'col')), may hold values from -6 to 6
- out_grad: bfloat16 [12288, 6144], P(('row', 'col')), may hold values from -0.125 to 0.125
- w_in: bfloat16 [6144, 48], replicated, may hold values from -0.078125 to 0.078125
- hidden_grad: bfloat16 [12288, 48], P(('row', 'col')), may hold values from -0.125 to 0.125
- qkv_grad: bfloat16 [12288, 64], P(('row', 'col')), may hold values from -0.125 to 0.125
- bucket_order: int32 [160], replicated, may hold values from 0 to 159, each once
Outputs:
- buckets: bfloat16 [160, 6144], replicated
Inputs may be any that keep to these rules, and one draw needn't show every extreme that they name: bucket_order is a permutation of 0 to 159.
All inputs are finite; a program needn't handle non-finite values.
Results may differ from a plain program's by a relative error of at most 0.0044.
Values may be sent and summed in bfloat16 or wider, within the bound.
A program may use at most 64 MiB of HBM per device.

v0:
```python
import jax
import jax.numpy as jnp
from jax import lax
from jax.sharding import PartitionSpec as P

NB = 4


def local(normed, out_grad, w_in, hidden_grad, qkv_grad, bucket_order):
    pre = jnp.dot(normed, w_in, preferred_element_type=jnp.float32)
    cdf = 0.5 * (1.0 + lax.erf(pre * 0.7071067811865476))
    pdf = jnp.exp(-0.5 * pre * pre) * 0.3989422804014327
    hidden = (pre * cdf).astype(jnp.bfloat16)
    pre_grad = (hidden_grad.astype(jnp.float32) * (cdf + pre * pdf)).astype(jnp.bfloat16)
    grad_qkv = jnp.dot(qkv_grad.T, normed, preferred_element_type=jnp.float32)
    grad_in = jnp.dot(pre_grad.T, normed, preferred_element_type=jnp.float32)
    grad_out = jnp.dot(hidden.T, out_grad, preferred_element_type=jnp.float32)
    stacked = jnp.concatenate([grad_qkv, grad_in, grad_out], axis=0)
    ordered = jnp.take(stacked, bucket_order, axis=0)
    per_bucket = ordered.shape[0] // NB
    results = []
    for bucket in range(NB):
        piece = ordered[bucket * per_bucket : (bucket + 1) * per_bucket]
        summed = lax.psum(piece, ("row", "col")).astype(jnp.bfloat16)
        results.append(summed)
    return jnp.concatenate(results, axis=0)


def solution(mesh):
    in_specs = (
        P(("row", "col"), None),
        P(("row", "col"), None),
        P(),
        P(("row", "col"), None),
        P(("row", "col"), None),
        P(),
    )
    out_specs = P()
    return jax.shard_map(local, mesh=mesh, in_specs=in_specs, out_specs=out_specs, check_vma=False)
```

profile of v0, /device:TPU:0, one launch (start us, length us, event | category | flops | bytes accessed | tf_op | source)
XLA Modules:
  0.0 118.2 jit_solution(10145399101433720630)
XLA Ops:
  0.0 0.0 copy-start
  0.0 0.0 copy-start.2
  0.0 1.1 copy-done
  1.1 4.3 %fusion.15 = f32[384,48]{0,1:T(8,128)S(1)} fusion(bf16[384,6144]{1,0:T(8,128)(2,1)} %param.6, bf16[6144,48]{0,1:T(8,128)(2,1)S(1)} %copy-done), kind=kOutput, calls=%fused_computation.24 | convolution fusion | flops 226492416 | bytes 5382144 | tf_op jit(solution)/shard_map/dot_general | solution.py:10
  5.4 0.0 copy-done.2
  5.4 0.0 copy-start.1
  5.4 0.0 copy-start.4
  5.4 0.9 fusion.6
  6.4 1.4 %copy-done.1 = bf16[384,6144]{1,0:T(8,128)(2,1)S(1)} copy-done((bf16[384,6144]{1,0:T(8,128)(2,1)S(1)}, bf16[384,6144]{1,0:T(8,128)(2,1)}, u32[]{:S(2)}) %copy-start.1) | copy-done | bytes 4718616
  7.7 0.0 copy-done.4
  7.7 0.0 copy-start.3
  7.7 0.9 fusion.7
  8.7 0.0 copy-done.3
  8.7 0.9 fusion.14
  9.6 0.0 copy-start.5
  9.7 2.1 %pad_maximum_fusion = f32[160,6144]{1,0:T(8,128)} fusion(f32[48,6144]{1,0:T(8,128)S(1)} %fusion.6, f32[48,6144]{1,0:T(8,128)S(1)} %fusion.7, f32[64,6144]{1,0:T(8,128)S(1)} %fusion.14), kind=kLoop, calls=%fused_computation.1 | loop fusion | flops 1966080 | bytes 7864320 | tf_op jit(solution)/shard_map/concatenate | solution.py:18
  11.8 0.0 copy-done.5
  11.8 7.4 %gather_fusion = f32[160,6144]{1,0:T(8,128)} fusion(f32[160,6144]{1,0:T(8,128)} %pad_maximum_fusion, s32[1024]{0:T(1024)S(1)} %pad_clamp_fusion), kind=kCustom, calls=%fused_computation | custom fusion | bytes 7864960 | tf_op jit(solution)/shard_map/jit(_take)/gather | solution.py:19
  19.3 2.7 %broadcast_select_fusion = f32[160,6144]{1,0:T(8,128)S(1)} fusion(f32[160,6144]{1,0:T(8,128)} %gather_fusion, pred[160]{0:T(512)(128)(4,1)S(1)} %compare_and_fusion), kind=kLoop, calls=%fused_computation.3 | loop fusion | flops 983040 | bytes 7864480 | tf_op jit(solution)/shard_map/jit(_take)/select_n | solution.py:19
  22.0 1.2 %fusion.13 = (f32[40,6144]{1,0:T(8,128)S(1)}, f32[40,6144]{1,0:T(8,128)S(1)}, f32[40,6144]{1,0:T(8,128)S(1)}, f32[40,6144]{1,0:T(8,128)}) fusion(f32[160,6144]{1,0:T(8,128)S(1)} %broadcast_select_fusion), kind=kLoop, calls=%fused_computation.22 | loop fusion | bytes 7864320 | tf_op jit(solution)/shard_map/slice | solution.py:23
  23.2 92.1 %all-reduce.2 = (bf16[40,6144]{1,0:T(8,128)(2,1)}, bf16[40,6144]{1,0:T(8,128)(2,1)}, bf16[40,6144]{1,0:T(8,128)(2,1)}, bf16[40,6144]{1,0:T(8,128)(2,1)}) all-reduce(f32[40,6144]{1,0:T(8,128)S(1)} %get-tuple-element.10, f32[40,6144]{1,0:T(8,128)S(1)} %get-tuple-element.11, ...), channel_id=1, replica_groups=mesh['row'=4,'col'=8] {'row','col'}, use_global_device_ids=true, to_apply=%region_3.4 | all-reduce | flops 983040 | bytes 5898240 | tf_op jit(solution)/shard_map/psum | solution.py:24
  115.3 2.9 %pad_maximum_fusion.1 = bf16[160,6144]{1,0:T(8,128)(2,1)} fusion(bf16[40,6144]{1,0:T(8,128)(2,1)} %get-tuple-element.5, bf16[40,6144]{1,0:T(8,128)(2,1)} %get-tuple-element.6, bf16[40,6144]{1,0:T(8,128)(2,1)} %get-tuple-element.7, bf16[40,6144]{1,0:T(8,128)(2,1)} %get-tuple-element.8), kind=kLoop, calls=%fused_computation.2 | loop fusion | flops 7864320 | bytes 3932160 | tf_op jit(solution)/shard_map/concatenate | solution.py:26
  (3 shorter events, 0.0 us)
Async XLA Ops:
  0.0 1.1 copy-start
  0.0 5.4 %copy-start.2 = (bf16[384,6144]{1,0:T(8,128)(2,1)S(1)}, bf16[384,6144]{1,0:T(8,128)(2,1)}, u32[]{:S(2)}) copy-start(bf16[384,6144]{1,0:T(8,128)(2,1)} %param.7) | copy-start | bytes 14155780
  5.4 2.3 %copy-start.1 = (bf16[384,6144]{1,0:T(8,128)(2,1)S(1)}, bf16[384,6144]{1,0:T(8,128)(2,1)}, u32[]{:S(2)}) copy-start(bf16[384,6144]{1,0:T(8,128)(2,1)} %param.6) | copy-start | bytes 14155780
  5.4 2.3 %copy-start.4 = (bf16[384,48]{0,1:T(8,128)(2,1)S(1)}, bf16[384,48]{0,1:T(8,128)(2,1)}, u32[]{:S(2)}) copy-start(bf16[384,48]{0,1:T(8,128)(2,1)} %param.9) | copy-start | bytes 110596
  7.7 0.9 copy-start.3
  9.6 2.2 %copy-start.5 = (s32[160]{0:T(256)S(1)}, s32[160]{0:T(256)}, u32[]{:S(2)}) copy-start(s32[160]{0:T(256)} %param.11) | copy-start | bytes 1924
where the time goes:
time: 118 us
  blocking collectives  92.1 us (78%)
  local copies, waits for them, and re-layouts  11.1 us (9%)
  other arithmetic  7.78 us (7%)
  matrix products  7.13 us (6%)
    psum x1, blocking collectives, local(): summed = lax.psum(piece, ('row', 'col')).astype(jnp.bfloat16)  92.1 us
    gather x1, local copies, waits for them, and re-layouts, local(): ordered = jnp.take(stacked, bucket_order, axis=0)  7.44 us
    dot_general x1, matrix products, local(): pre = jnp.dot(normed, w_in, preferred_element_type=jnp.float32)  4.31 us
    concatenate x1, other arithmetic, local(): return jnp.concatenate(results, axis=0)  2.92 us
    select_n x2, other arithmetic, local(): ordered = jnp.take(stacked, bucket_order, axis=0)  2.7 us
    unnamed x12, local copies, waits for them, and re-layouts  2.46 us

commit v1 on v0

--- a/solution.py
+++ b/solution.py
@@ -4,6 +4,12 @@
 from jax.sharding import PartitionSpec as P
 
 NB = 4
+
+
+def quarters_write(xx):
+    extra = jax.lax.psum(xx, "row")
+    heard = jax.lax.psum(extra, "col")
+    return heard
 
 
 def local(normed, out_grad, w_in, hidden_grad, qkv_grad, bucket_order):
@@ -21,7 +27,7 @@
     results = []
     for bucket in range(NB):
         piece = ordered[bucket * per_bucket : (bucket + 1) * per_bucket]
-        summed = lax.psum(piece, ("row", "col")).astype(jnp.bfloat16)
+        summed = quarters_write(piece).astype(jnp.bfloat16)
         results.append(summed)
     return jnp.concatenate(results, axis=0)
 

time: 118 us -> 280 us (2.37)
  waiting for transfers between devices: 0 us -> 84.2 us
  blocking collectives: 92.1 us -> 157 us
  between operations: 0.08 us -> 13.5 us
    psum x0 -> x1, waiting for transfers between devices: none -> 84.2 us  [quarters_write(): extra = jax.lax.psum(xx, 'row')]
    psum x1, blocking collectives: 92.1 us -> 157 us  [quarters_write(): heard = jax.lax.psum(extra, 'col')]
  transfers between devices with their start and end apart: 0 -> 1, of which waited for: 0 -> 1; matrix products, arithmetic and copies ran while one was open for 0% -> 0% of each run, Pallas kernels for 0% -> 0%
where the time goes in v1:
time: 280 us
  blocking collectives  157 us (56%)
  waiting for transfers between devices  84.2 us (30%)
  between operations  13.5 us (5%)
  local copies, waits for them, and re-layouts  10.8 us (4%)
  other arithmetic  8.19 us (3%)
  matrix products  6.64 us (2%)
    psum x1, blocking collectives, quarters_write(): heard = jax.lax.psum(extra, 'col')  157 us
    psum x1, waiting for transfers between devices, quarters_write(): extra = jax.lax.psum(xx, 'row')  84.2 us
    gather x1, local copies, waits for them, and re-layouts, local(): ordered = jnp.take(stacked, bucket_order, axis=0)  7.44 us
  transfers between devices with their start and end apart: 1, of which 1 were waited for; matrix products, arithmetic and copies ran while one was open for 0% of the time, Pallas kernels for 0%

profile of v1, /device:TPU:0, one launch (start us, length us, event | category | flops | bytes accessed | tf_op | source)
XLA Modules:
  0.0 280.1 jit_solution(4870922449635941462)
XLA Ops:
  6.5 0.0 copy-start
  6.5 0.0 all-reduce.5.cloned.1.call-start
  6.5 0.0 copy-start.2
  6.5 0.8 compare_select_fusion
  7.4 1.1 compare_and_fusion
  8.5 0.0 copy-done
  8.5 3.8 %fusion.15 = f32[384,48]{0,1:T(8,128)S(1)} fusion(bf16[384,6144]{1,0:T(8,128)(2,1)} %param.6, bf16[6144,48]{0,1:T(8,128)(2,1)S(1)} %copy-done), kind=kOutput, calls=%fused_computation.24 | convolution fusion | flops 226492416 | bytes 5382144 | tf_op jit(solution)/shard_map/dot_general | solution.py:16
  12.3 0.0 copy-done.2
  12.3 0.0 copy-start.1
  12.3 0.0 copy-start.4
  12.3 0.9 fusion.6
  13.3 1.4 copy-done.1
  14.6 0.0 copy-done.4
  14.6 0.0 copy-start.3
  14.6 0.9 fusion.7
  15.6 0.0 copy-done.3
  15.6 0.9 fusion.14
  16.6 2.2 pad_maximum_fusion
  18.7 7.4 %gather_fusion = f32[160,6144]{1,0:T(8,128)} fusion(f32[160,6144]{1,0:T(8,128)} %pad_maximum_fusion, s32[1024]{0:T(1024)S(1)} %pad_clamp_fusion), kind=kCustom, calls=%fused_computation | custom fusion | bytes 7864960 | tf_op jit(solution)/shard_map/jit(_take)/gather | solution.py:25
  26.2 2.7 broadcast_select_fusion
  28.9 2.0 fusion.13
  30.9 0.0 all-reduce.5.cloned.1.call-update
  30.9 84.2 %all-reduce.5.cloned.1.call-done = (f32[40,6144]{1,0:T(8,128)}, f32[40,6144]{1,0:T(8,128)}, f32[40,6144]{1,0:T(8,128)}, f32[40,6144]{1,0:T(8,128)}) async-done(((f32[40,6144]{1,0:T(8,128)}, f32[40,6144]{1,0:T(8,128)}, f32[40,6144]{1,0:T(8,128)}, f32[40,6144]{1,0:T(8,128)}), (f32[40,6144]{1,0:T(8,128)}, f32[40,6144]{1,0:T(8,128)}, f32[40,6144]{1,0:T(8,128)}, ...) | async-done | bytes 3932176 | tf_op jit(solution)/shard_map/psum | solution.py:10
  115.1 156.8 %all-reduce.6 = (bf16[40,6144]{1,0:T(8,128)(2,1)S(1)}, bf16[40,6144]{1,0:T(8,128)(2,1)S(1)}, bf16[40,6144]{1,0:T(8,128)(2,1)S(1)}, bf16[40,6144]{1,0:T(8,128)(2,1)S(1)}) all-reduce(f32[40,6144]{1,0:T(8,128)} %get-tuple-element.9, f32[40,6144]{1,0:T(8,128)} %get-tuple-element.10, ...), channel_id=1, replica_groups=mesh['row'=4,'col'=8] {'col'}, use_global_device_ids=true, to_apply=%region_7.8 | all-reduce | flops 983040 | bytes 5898240 | tf_op jit(solution)/shard_map/psum | solution.py:11
  271.9 1.4 pad_maximum_fusion.1
  (1 shorter events, 0.0 us)
Async XLA Ops:
  6.5 1.9 copy-start
  6.5 108.5 %all-reduce.5.cloned.1.call-start = ((), (), s32[]{:S(2)}) async-start(), calls=%async_computation | async-start | bytes 7864320 | tf_op jit(solution)/shard_map/psum | solution.py:10
  6.5 5.8 %copy-start.2 = (bf16[384,6144]{1,0:T(8,128)(2,1)S(1)}, bf16[384,6144]{1,0:T(8,128)(2,1)}, u32[]{:S(2)}) copy-start(bf16[384,6144]{1,0:T(8,128)(2,1)} %param.7) | copy-start | bytes 14155780
  12.3 2.3 copy-start.1
  12.3 2.3 copy-start.4
  14.6 0.9 copy-start.3
Sparse Core Ops, SparseCore 0:
  31.0 83.9 all-reduce.4
